TPU v7x, 32 devices: a whole 2x2x4 slice. The times are simulated.
32 devices in a mesh: groups: 2 (over y), expert: 8 (over z, x), tensor: 2 (over core).
Axes of the slice: x: 2, y: 2, z: 4, core: 2. Of those that a mesh axis runs over, the one named last changes fastest.
Arguments:
- tokens: bfloat16 [1024, 1536], P(('groups', 'expert')), parts along dimension 0, may hold values from -12 to 12
- gain: float32 [1536], replicated, may hold values from 0.25 to 1.75
- route_ids: int32 [1024, 4], P(('groups', 'expert')), parts along dimension 0, may hold values from 0 to 3, as said below
- route_weights: float32 [1024, 4], P(('groups', 'expert')), parts along dimension 0, may hold values from 0.05 to 0.5
- w_gate: bfloat16 [8, 1536, 768], P('expert', None, 'tensor'), may hold values from -0.15625 to 0.15625
- w_up: bfloat16 [8, 1536, 768], P('expert', None, 'tensor'), may hold values from -0.15625 to 0.15625
- w_down: bfloat16 [8, 768, 1536], P('expert', 'tensor'), may hold values from -0.15625 to 0.15625
Outputs:
- mixed: bfloat16 [1024, 1536], P(('groups', 'expert')), parts along dimension 0
There are 2 independent parts, one for each index of `groups`. A program takes and returns all parts, laid end to end along the dimension named above; an argument that names none is the same for every part. Nothing has to cross between parts.
Inputs may be any that keep to these rules, and one draw needn't show every extreme that they name: `route_ids`: each row names 4 different experts. In each aligned block of 32 rows no expert is named more than 32 times; one expert, the same in every block, is named exactly 32 times in every block, and the other experts' counts within a block differ by at most one.
All inputs are finite; a program needn't handle non-finite values.
Results may differ from a plain program's by a relative error of at most 0.0045.
Values may be sent and summed in bfloat16 or wider, within the bound.
A program may use at most 64 MiB of HBM per device.

v0:
```python
import jax
import jax.numpy as jnp
from jax import lax
from jax.sharding import PartitionSpec as P


def gated_unit(gate_val, up_val):
    return gate_val * jax.nn.sigmoid(1.702 * gate_val) * (up_val + 1.0)


def route_tables(chosen_ids, chosen_weights, expert_count, slot_room):
    row_count, top_count = chosen_ids.shape
    matches = (chosen_ids[:, :, None] == jnp.arange(expert_count, dtype=jnp.int32)).astype(
        jnp.float32
    )
    flat_match = matches.reshape(row_count * top_count, expert_count)
    order_range = jnp.arange(row_count * top_count, dtype=jnp.int32)
    earlier = (order_range[:, None] > order_range[None, :]).astype(jnp.float32)
    before = jnp.dot(
        earlier, flat_match, precision=lax.Precision.HIGHEST, preferred_element_type=jnp.float32
    )
    position = jnp.sum(before * flat_match, axis=1).reshape(row_count, top_count).astype(jnp.int32)
    slot_index = chosen_ids * slot_room + position
    targets = jnp.arange(expert_count * slot_room, dtype=jnp.int32)
    slot_hits = slot_index[None, :, :] == targets[:, None, None]
    send_table = jnp.sum(slot_hits.astype(jnp.float32), axis=2).astype(jnp.bfloat16)
    mix_table = jnp.sum(jnp.where(slot_hits, chosen_weights[None, :, :], 0.0), axis=2)
    return (send_table, mix_table)


def per_device(tokens, gain, route_ids, route_weights, w_gate, w_up, w_down):
    expert_axis = lax.axis_size("expert")
    expert_count = expert_axis // 2
    tensor_count = lax.axis_size("tensor")
    own_rows = tokens.shape[0] // tensor_count
    top_count = route_ids.shape[1]
    capacity = max(2, own_rows * top_count // expert_count)
    gate_local = w_gate[0]
    up_local = w_up[0]
    down_local = w_down[0]
    first_row = lax.axis_index("tensor") * own_rows
    own_tokens = lax.dynamic_slice_in_dim(tokens, first_row, own_rows, 0)
    own_ids = lax.dynamic_slice_in_dim(route_ids, first_row, own_rows, 0)
    own_weights = lax.dynamic_slice_in_dim(route_weights, first_row, own_rows, 0)
    resident = own_tokens.astype(jnp.float32)
    inv_rms = lax.rsqrt(jnp.mean(resident * resident, axis=1, keepdims=True) + 1e-05)
    normed = (resident * inv_rms * gain).astype(jnp.bfloat16)
    send_table, mix_table = route_tables(own_ids, own_weights, expert_count, capacity)
    packed = jnp.dot(send_table, normed, preferred_element_type=jnp.float32).astype(jnp.bfloat16)
    features = packed.shape[1]
    by_expert = packed.reshape(expert_count, 1, capacity, features)
    outgoing = jnp.broadcast_to(by_expert, (expert_count, 2, capacity, features)).reshape(
        expert_axis * capacity, features
    )
    arrived = lax.all_to_all(outgoing, "expert", split_axis=0, concat_axis=0, tiled=True)
    row_piece = lax.all_gather(arrived, "tensor", axis=0, tiled=True)
    gate_val = jnp.dot(row_piece, gate_local, preferred_element_type=jnp.float32)
    up_val = jnp.dot(row_piece, up_local, preferred_element_type=jnp.float32)
    hidden = gated_unit(gate_val, up_val).astype(jnp.bfloat16)
    partial_value = lax.psum_scatter(
        jnp.dot(hidden, down_local, preferred_element_type=jnp.float32),
        "tensor",
        scatter_dimension=0,
        tiled=True,
    )
    returned = lax.all_to_all(
        partial_value.astype(jnp.bfloat16), "expert", split_axis=0, concat_axis=0, tiled=True
    ).astype(partial_value.dtype)
    expert_out = (
        returned.reshape(expert_count, 2, capacity, features)
        .sum(axis=1)
        .reshape(expert_count * capacity, features)
    )
    weighted = jnp.dot(
        mix_table.T, expert_out, precision=lax.Precision.HIGHEST, preferred_element_type=jnp.float32
    )
    finished = (resident + weighted).astype(jnp.bfloat16)
    return lax.all_gather(finished, "tensor", axis=0, tiled=True)


def solution(mesh):
    placed = (
        P(("groups", "expert"), None),
        P(),
        P(("groups", "expert"), None),
        P(("groups", "expert"), None),
        P("expert", None, "tensor"),
        P("expert", None, "tensor"),
        P("expert", "tensor", None),
    )
    return jax.shard_map(
        per_device,
        mesh=mesh,
        in_specs=placed,
        out_specs=P(("groups", "expert"), None),
        check_vma=False,
    )
```

profile of v0, /device:TPU:0, one launch (start us, length us, event | category | flops | bytes accessed | tf_op | source)
XLA Modules:
  0.0 106.2 jit_solution(7419597730249863763)
XLA Ops:
  6.5 0.0 copy-start
  6.5 0.0 all-gather.2.cloned.1.call-start
  6.5 1.1 %fusion.18 = f32[32]{0:T(128)S(1)} fusion(bf16[64,1536]{1,0:T(8,128)(2,1)} %param.7, s32[]{:T(128)S(6)} %select_n.9), kind=kLoop, calls=%fused_computation.24 | loop fusion | flops 147424 | bytes 98436 | tf_op jit(solution)/shard_map/reduce_sum | solution.py:46
  7.7 0.8 constant_dynamic-slice_fusion.1
  8.4 0.8 constant_dynamic-slice_fusion
  9.2 0.1 copy.14
  9.3 0.1 eq.30
  9.4 0.1 fusion.9
  9.5 0.1 convert_element_type.42
  9.7 0.1 copy.13
  9.7 0.1 convert_reduce_fusion.1
  9.9 1.2 %convolution_convert_fusion = bf16[128,1536]{1,0:T(8,128)(2,1)S(1)} fusion(f32[1536]{0:T(1024)} %param.8, f32[32]{0:T(128)S(1)} %add_rsqrt_fusion, bf16[64,1536]{1,0:T(8,128)(2,1)} %param.7, s32[]{:T(128)S(6)} %select_n.9, bf16[128,32]{0,1:T(8,128)(2,1)S(1)} %get-tuple-element.5), kind=kOutput, calls=%fused_computation | convolution fusion | flops 12976128 | bytes 508036 | tf_op jit(solution)/shard_map/dot_general | solution.py:49
  11.1 0.1 broadcast_in_dim.19
  11.2 27.3 %all_to_all.21 = bf16[8,32,1536]{2,1,0:T(8,128)(2,1)} all-to-all(bf16[8,32,1536]{2,1,0:T(8,128)(2,1)S(1)} %bitcast.25), channel_id=1, replica_groups=mesh['groups'=2,'expert'=8,'tensor'=2] {'expert'}, dimensions={0} | all-to-all | bytes 1572864 | tf_op jit(solution)/shard_map/all_to_all | solution.py:55
  38.5 0.0 all-gather.2.cloned.1.call-update
  38.5 0.0 reduce-scatter.2.cloned.1.call-start
  38.6 9.0 %all-gather.2.cloned.1.call-done = bf16[512,1536]{1,0:T(8,128)(2,1)} async-done(((bf16[256,1536]{1,0:T(8,128)(2,1)}), bf16[512,1536]{1,0:T(8,128)(2,1)}) %all-gather.2.cloned.1.call-update) | async-done | bytes 1572880 | tf_op jit(solution)/shard_map/all_gather | solution.py:56
  47.5 0.0 copy-start.2
  47.5 2.8 %fusion.7 = f32[512,384]{1,0:T(8,128)S(1)} fusion(bf16[512,1536]{1,0:T(8,128)(2,1)} %all-gather.2.cloned.1.call-done, bf16[1,1536,384]{2,1,0:T(8,128)(2,1)} %param.11), kind=kOutput, calls=%fused_computation.10 | convolution fusion | flops 603979776 | bytes 3538944 | tf_op jit(solution)/shard_map/dot_general | solution.py:57
  50.4 0.0 copy-done
  50.4 0.0 copy-done.2
  50.4 4.8 %fusion.3 = f32[512,1536]{1,0:T(8,128)} fusion(bf16[512,1536]{1,0:T(8,128)(2,1)S(1)} %copy-done.2, bf16[1,384,1536]{2,1,0:T(8,128)(2,1)S(1)} %copy-done, bf16[1,1536,384]{2,1,0:T(8,128)(2,1)} %param.12, f32[512,384]{1,0:T(8,128)S(1)} %fusion.7), kind=kOutput, calls=%fused_computation.7 | convolution fusion | flops 1209532416 | bytes 7864320 | tf_op jit(solution)/shard_map/dot_general | solution.py:61
  55.1 0.0 reduce-scatter.2.cloned.1.call-update
  55.2 12.5 %reduce-scatter.2.cloned.1.call-done = f32[256,1536]{1,0:T(8,128)} async-done(((f32[512,1536]{1,0:T(8,128)}), f32[256,1536]{1,0:T(8,128)}) %reduce-scatter.2.cloned.1.call-update) | async-done | bytes 1572880 | tf_op jit(solution)/shard_map/reduce_scatter | solution.py:60
  67.7 1.5 %convert_element_type.48 = bf16[256,1536]{1,0:T(8,128)(2,1)S(1)} convert(f32[256,1536]{1,0:T(8,128)} %reduce-scatter.2.cloned.1.call-done) | non-fusion elementwise | flops 393216 | bytes 2359296 | tf_op jit(solution)/shard_map/convert_element_type | solution.py:67
  69.1 26.1 %all_to_all.22 = bf16[8,32,1536]{2,1,0:T(8,128)(2,1)S(1)} all-to-all(bf16[8,32,1536]{2,1,0:T(8,128)(2,1)S(1)} %bitcast.26), channel_id=1, replica_groups=mesh['groups'=2,'expert'=8,'tensor'=2] {'expert'}, dimensions={0} | all-to-all | bytes 1572864 | tf_op jit(solution)/shard_map/all_to_all | solution.py:66
  95.3 0.0 copy-start.1
  95.3 0.1 convert_reduce_fusion
  95.4 0.8 copy-done.1
  96.2 0.5 fusion
  96.7 1.9 %all_gather.7 = bf16[64,1536]{1,0:T(8,128)(2,1)S(1)} all-gather(bf16[32,1536]{1,0:T(8,128)(2,1)S(1)} %fusion), channel_id=1, replica_groups=mesh['groups'=2,'expert'=8,'tensor'=2] {'tensor'}, dimensions={0}, use_global_device_ids=true | all-gather | bytes 294912 | tf_op jit(solution)/shard_map/all_gather | solution.py:78
  98.7 0.7 copy.16
  (3 shorter events, 0.0 us)
Async XLA Ops:
  6.5 43.8 %copy-start = (bf16[1,384,1536]{2,1,0:T(8,128)(2,1)S(1)}, bf16[1,384,1536]{2,1,0:T(8,128)(2,1)}, u32[]{:S(2)}) copy-start(bf16[1,384,1536]{2,1,0:T(8,128)(2,1)} %param.13) | copy-start | bytes 3538948
  6.5 41.0 %all-gather.2.cloned.1.call-start = ((), (), s32[]{:S(2)}) async-start(), calls=%async_computation.3 | async-start | bytes 2359296 | tf_op jit(solution)/shard_map/all_gather | solution.py:56
  38.5 29.1 %reduce-scatter.2.cloned.1.call-start = ((), (), s32[]{:S(2)}) async-start(), calls=%async_computation.4 | async-start | bytes 4718592 | tf_op jit(solution)/shard_map/reduce_scatter | solution.py:60
  47.5 2.9 %copy-start.2 = (bf16[512,1536]{1,0:T(8,128)(2,1)S(1)}, bf16[512,1536]{1,0:T(8,128)(2,1)}, u32[]{:S(2)}) copy-start(bf16[512,1536]{1,0:T(8,128)(2,1)} %all-gather.2.cloned.1.call-done) | copy-start | bytes 4718596
  95.3 0.9 copy-start.1
Sparse Core Ops, SparseCore 0:
  38.6 8.8 all-gather.1
  55.3 12.3 reduce-scatter.1
where the time goes:
time: 107 us; the launch traced here: 106 us
  blocking collectives  55.4 us (52%)
  waiting for transfers between devices  21.5 us (20%)
  between operations  13.5 us (13%)
  matrix products  9.5 us (9%)
  local copies, waits for them, and re-layouts  3.43 us (3%)
  other arithmetic  2.86 us (3%)
    all_to_all x1, blocking collectives, per_device(): lax.all_to_all(outgoing, 'expert', split_axis=0, concat_axis=0, tiled=True)  27.3 us
    all_to_all x1, blocking collectives, per_device(): lax.all_to_all(partial_value.astype(jnp.bfloat16), 'expert', split_axis=0...  26.1 us
    reduce_scatter x1, waiting for transfers between devices, per_device(): lax.psum_scatter(jnp.dot(hidden, down_local, preferred_element_type=jnp.f...  12.5 us
    all_gather x1, waiting for transfers between devices, per_device(): row_piece = lax.all_gather(arrived, 'tensor', axis=0, tiled=True)  8.95 us
    dot_general x1, matrix products, per_device(): jnp.dot(hidden, down_local, preferred_element_type=jnp.float32)  4.78 us
    dot_general x1, matrix products, per_device(): jnp.dot(row_piece, gate_local, preferred_element_type=jnp.float32)  2.83 us
  transfers between devices with their start and end apart: 2, of which 2 were waited for; matrix products, arithmetic and copies ran while one was open for 0% of the time, Pallas kernels for 0%

commit v1 on v0

--- a/solution.py
+++ b/solution.py
@@ -53,7 +53,8 @@
         expert_axis * capacity, features
     )
     arrived = lax.all_to_all(outgoing, "expert", split_axis=0, concat_axis=0, tiled=True)
-    row_piece = lax.all_gather(arrived, "tensor", axis=0, tiled=True)
+    sent = jnp.stack([arrived] * lax.axis_size("tensor"))
+    row_piece = jnp.concatenate(lax.all_to_all(sent, "tensor", 0, 0), axis=0)
     gate_val = jnp.dot(row_piece, gate_local, preferred_element_type=jnp.float32)
     up_val = jnp.dot(row_piece, up_local, preferred_element_type=jnp.float32)
     hidden = gated_unit(gate_val, up_val).astype(jnp.bfloat16)

time: 107 us -> 98.1 us (0.917)
  waiting for transfers between devices: 21.5 us -> 10.4 us
  blocking collectives: 55.4 us -> 60.6 us
  matrix products: 9.5 us -> 7.65 us
    all_gather x1 -> x0, waiting for transfers between devices: 8.95 us -> none  [per_device(): row_piece = lax.all_gather(arrived, 'tensor', axis=0, tiled=True)]
    all_to_all x0 -> x1, blocking collectives: none -> 5.13 us  [per_device(): row_piece = jnp.concatenate(lax.all_to_all(sent, 'tensor', 0, 0), axis=0)]
    reduce_scatter x1, waiting for transfers between devices: 12.5 us -> 10.4 us  [per_device(): lax.psum_scatter(jnp.dot(hidden, down_local, preferred_element_type=jnp.f...]
    dot_general x1, matrix products: 2.83 us -> 0.97 us  [per_device(): jnp.dot(row_piece, gate_local, preferred_element_type=jnp.float32)]
  transfers between devices with their start and end apart: 2 -> 1, of which waited for: 2 -> 1; matrix products, arithmetic and copies ran while one was open for 0% -> 0% of each run, Pallas kernels for 0% -> 0%
where the time goes in v1:
time: 98.1 us; the launch traced here: 97.7 us
  blocking collectives  60.6 us (62%)
  between operations  13.5 us (14%)
  waiting for transfers between devices  10.4 us (11%)
  matrix products  7.65 us (8%)
  other arithmetic  3 us (3%)
  local copies, waits for them, and re-layouts  2.64 us (3%)
    all_to_all x1, blocking collectives, per_device(): lax.all_to_all(outgoing, 'expert', split_axis=0, concat_axis=0, tiled=True)  27.2 us
    all_to_all x1, blocking collectives, per_device(): lax.all_to_all(partial_value.astype(jnp.bfloat16), 'expert', split_axis=0...  26.3 us
    reduce_scatter x1, waiting for transfers between devices, per_device(): lax.psum_scatter(jnp.dot(hidden, down_local, preferred_element_type=jnp.f...  10.4 us
    all_to_all x1, blocking collectives, per_device(): row_piece = jnp.concatenate(lax.all_to_all(sent, 'tensor', 0, 0), axis=0)  5.13 us
    dot_general x1, matrix products, per_device(): jnp.dot(hidden, down_local, preferred_element_type=jnp.float32)  4.77 us
  transfers between devices with their start and end apart: 1, of which 1 were waited for; matrix products, arithmetic and copies ran while one was open for 0% of the time, Pallas kernels for 0%

profile of v1, /device:TPU:0, one launch (start us, length us, event | category | flops | bytes accessed | tf_op | source)
XLA Modules:
  0.0 97.7 jit_solution(5081696575463794640)
XLA Ops:
  6.5 0.0 copy-start
  6.5 0.0 reduce-scatter.2.cloned.1.call-start
  6.5 1.1 %fusion.18 = f32[32]{0:T(128)S(1)} fusion(bf16[64,1536]{1,0:T(8,128)(2,1)} %param.7, s32[]{:T(128)S(6)} %select_n.9), kind=kLoop, calls=%fused_computation.25 | loop fusion | flops 147424 | bytes 98436 | tf_op jit(solution)/shard_map/reduce_sum | solution.py:46
  7.7 0.8 constant_dynamic-slice_fusion.1
  8.4 0.8 constant_dynamic-slice_fusion
  9.2 0.1 copy.14
  9.3 0.1 eq.30
  9.4 0.1 fusion.9
  9.5 0.1 convert_element_type.42
  9.7 0.1 copy.13
  9.7 0.1 convert_reduce_fusion.1
  9.9 1.2 %convolution_convert_fusion = bf16[128,1536]{1,0:T(8,128)(2,1)S(1)} fusion(f32[1536]{0:T(1024)} %param.8, f32[32]{0:T(128)S(1)} %add_rsqrt_fusion, bf16[64,1536]{1,0:T(8,128)(2,1)} %param.7, s32[]{:T(128)S(6)} %select_n.9, bf16[128,32]{0,1:T(8,128)(2,1)S(1)} %get-tuple-element.5), kind=kOutput, calls=%fused_computation | convolution fusion | flops 12976128 | bytes 508036 | tf_op jit(solution)/shard_map/dot_general | solution.py:49
  11.1 0.1 broadcast_in_dim.19
  11.2 27.2 %all_to_all.23 = bf16[8,32,1536]{2,1,0:T(8,128)(2,1)S(1)} all-to-all(bf16[8,32,1536]{2,1,0:T(8,128)(2,1)S(1)} %bitcast.25), channel_id=1, replica_groups=mesh['groups'=2,'expert'=8,'tensor'=2] {'expert'}, dimensions={0} | all-to-all | bytes 1572864 | tf_op jit(solution)/shard_map/all_to_all | solution.py:55
  38.4 0.1 pad_maximum_fusion
  38.5 0.0 copy-start.2
  38.5 5.1 %all_to_all.24 = bf16[2,256,1536]{2,1,0:T(8,128)(2,1)S(1)} all-to-all(bf16[2,256,1536]{2,1,0:T(8,128)(2,1)S(1)} %pad_maximum_fusion), channel_id=1, replica_groups=mesh['groups'=2,'expert'=8,'tensor'=2] {'tensor'}, dimensions={0} | all-to-all | bytes 3145728 | tf_op jit(solution)/shard_map/all_to_all | solution.py:57
  43.7 0.0 copy-done.2
  43.7 1.0 fusion.7
  44.6 0.0 copy-done
  44.7 4.8 %fusion.3 = f32[512,1536]{1,0:T(8,128)} fusion(bf16[512,1536]{1,0:T(8,128)(2,1)S(1)} %bitcast.29, bf16[1,384,1536]{2,1,0:T(8,128)(2,1)S(1)} %copy-done, bf16[1,1536,384]{2,1,0:T(8,128)(2,1)} %param.12, f32[512,384]{1,0:T(8,128)S(1)} %fusion.7), kind=kOutput, calls=%fused_computation.8 | convolution fusion | flops 1209532416 | bytes 7864320 | tf_op jit(solution)/shard_map/dot_general | solution.py:62
  49.4 0.0 reduce-scatter.2.cloned.1.call-update
  49.5 10.4 %reduce-scatter.2.cloned.1.call-done = f32[256,1536]{1,0:T(8,128)} async-done(((f32[512,1536]{1,0:T(8,128)}), f32[256,1536]{1,0:T(8,128)}) %reduce-scatter.2.cloned.1.call-update) | async-done | bytes 1572880 | tf_op jit(solution)/shard_map/reduce_scatter | solution.py:61
  59.8 1.5 %convert_element_type.48 = bf16[256,1536]{1,0:T(8,128)(2,1)S(1)} convert(f32[256,1536]{1,0:T(8,128)} %reduce-scatter.2.cloned.1.call-done) | non-fusion elementwise | flops 393216 | bytes 2359296 | tf_op jit(solution)/shard_map/convert_element_type | solution.py:68
  61.3 0.0 copy-start.1
  61.3 26.3 %all_to_all.25 = bf16[8,32,1536]{2,1,0:T(8,128)(2,1)S(1)} all-to-all(bf16[8,32,1536]{2,1,0:T(8,128)(2,1)S(1)} %bitcast.27), channel_id=1, replica_groups=mesh['groups'=2,'expert'=8,'tensor'=2] {'expert'}, dimensions={0} | all-to-all | bytes 1572864 | tf_op jit(solution)/shard_map/all_to_all | solution.py:67
  87.6 0.1 convert_reduce_fusion
  87.7 0.0 copy-done.1
  87.7 0.5 fusion
  88.2 1.9 %all_gather.3 = bf16[64,1536]{1,0:T(8,128)(2,1)S(1)} all-gather(bf16[32,1536]{1,0:T(8,128)(2,1)S(1)} %fusion), channel_id=1, replica_groups=mesh['groups'=2,'expert'=8,'tensor'=2] {'tensor'}, dimensions={0}, use_global_device_ids=true | all-gather | bytes 294912 | tf_op jit(solution)/shard_map/all_gather | solution.py:79
  90.2 0.7 copy.16
  (3 shorter events, 0.0 us)
Async XLA Ops:
  6.5 38.1 %copy-start = (bf16[1,384,1536]{2,1,0:T(8,128)(2,1)S(1)}, bf16[1,384,1536]{2,1,0:T(8,128)(2,1)}, u32[]{:S(2)}) copy-start(bf16[1,384,1536]{2,1,0:T(8,128)(2,1)} %param.13) | copy-start | bytes 3538948
  6.5 53.3 %reduce-scatter.2.cloned.1.call-start = ((), (), s32[]{:S(2)}) async-start(), calls=%async_computation.4 | async-start | bytes 4718592 | tf_op jit(solution)/shard_map/reduce_scatter | solution.py:61
  38.5 5.1 %copy-start.2 = (bf16[1,1536,384]{2,1,0:T(8,128)(2,1)S(1)}, bf16[1,1536,384]{2,1,0:T(8,128)(2,1)}, u32[]{:S(2)}) copy-start(bf16[1,1536,384]{2,1,0:T(8,128)(2,1)} %param.11) | copy-start | bytes 3538948
  61.3 26.4 %copy-start.1 = (bf16[64,1536]{1,0:T(8,128)(2,1)S(1)}, bf16[64,1536]{1,0:T(8,128)(2,1)}, u32[]{:S(2)}) copy-start(bf16[64,1536]{1,0:T(8,128)(2,1)} %param.7) | copy-start | bytes 589828
Sparse Core Ops, SparseCore 0:
  49.6 10.1 reduce-scatter.1
